TPU v7x, 256 devices: a whole 4x4x8 slice. The times are simulated.
256 devices in a mesh: row: 8 (over y, z_lo), col: 32 (over x, z_hi, core).
Axes of the slice: x: 4, y: 4, z: 8 (z_hi: 4, z_lo: 2; z = z_hi * 2 + z_lo), core: 2. Of those that a mesh axis runs over, the one named last changes fastest.
Arguments:
- x_field: bfloat16 [131072, 256], P('col'), may hold values from -6 to 6
- observed: bfloat16 [8192, 256], P(('row', 'col')), may hold values from -6 to 6
- sat_scale: float32 [256], replicated, may hold values from 0.5 to 4
- u_coef: bfloat16 [16, 256, 512, 256], P('row', 'col'), may hold values from -0.03125 to 0.03125
- v_coef: bfloat16 [16, 256, 512, 256], P('row', 'col'), may hold values from -0.25 to 0.25
- ranks: int32 [16, 256], P('row', 'col'), may hold values from 16 to 256
Outputs:
- gradient: bfloat16 [131072, 256], P('col')
All inputs are finite; a program needn't handle non-finite values.
Results may differ from a plain program's by a relative error of at most 0.0065.
Values may be sent and summed in bfloat16 or wider, within the bound.
A program may use at most 64 MiB of HBM per device.

v0:
```python
import jax
import jax.numpy as jnp
from jax import lax
from jax.sharding import PartitionSpec as P


def in_blocks(shard, dim, count):
    before, after = (shard.shape[:dim], shard.shape[dim + 1 :])
    return jnp.moveaxis(shard.reshape(*before, count, -1, *after), dim, 0)


def sent_and_summed(shard, axis, dim):
    blocks = in_blocks(shard, dim, lax.axis_size(axis))
    arrived = lax.all_to_all(blocks, axis, split_axis=0, concat_axis=0, tiled=True)
    return arrived.sum(axis=0)


def in_order(blocks, dim):
    blocks = jnp.moveaxis(blocks, 0, dim)
    dims = blocks.shape
    return blocks.reshape(*dims[:dim], dims[dim] * dims[dim + 1], *dims[dim + 2 :])


def sent_to_all(shard, axis):
    copies = jnp.broadcast_to(shard, (lax.axis_size(axis), *shard.shape))
    return lax.all_to_all(copies, axis, split_axis=0, concat_axis=0, tiled=True)


def gather_directly(shard, axis, dim):
    return in_order(sent_to_all(shard, axis), dim)


def saturate(predicted, observed, sat_scale):
    misfit = (predicted - observed.astype(jnp.float32)) / sat_scale
    return (sat_scale * jnp.tanh(misfit)).astype(jnp.bfloat16)


def local(x_field, observed, sat_scale, u_coef, v_coef, ranks):
    tile_rows, tile_cols, tile_width, rank_cap = u_coef.shape
    sources = x_field.shape[1]
    rank_mask = (lax.broadcasted_iota(jnp.int32, (1, 1, rank_cap), 2) < ranks[:, :, None]).astype(
        jnp.float32
    )[..., None]
    source_tiles = x_field.reshape(tile_cols, tile_width, sources)
    coeffs = jnp.einsum("ajtk,jts->ajks", v_coef, source_tiles, preferred_element_type=jnp.float32)
    coeffs = (coeffs * rank_mask).astype(jnp.bfloat16)
    predicted = jnp.einsum("ajtk,ajks->ats", u_coef, coeffs, preferred_element_type=jnp.float32)
    predicted = predicted.reshape(tile_rows * tile_width, sources)
    forward_share = sent_and_summed(predicted, "col", 0)
    resid_share = saturate(forward_share, observed, sat_scale)
    group_resid = gather_directly(resid_share, "col", 0)
    resid_tiles = group_resid.reshape(tile_rows, tile_width, sources)
    adjoint = jnp.einsum("ajtk,ats->ajks", u_coef, resid_tiles, preferred_element_type=jnp.float32)
    adjoint = (adjoint * rank_mask).astype(jnp.bfloat16)
    partial_grad = jnp.einsum("ajtk,ajks->jts", v_coef, adjoint, preferred_element_type=jnp.float32)
    partial_grad = partial_grad.reshape(tile_cols * tile_width, sources)
    grad_share = sent_and_summed(partial_grad, "row", 0).astype(jnp.bfloat16)
    gradient = gather_directly(grad_share, "row", 0)
    return gradient


def solution(mesh):
    return jax.shard_map(
        local,
        mesh=mesh,
        in_specs=(
            P("col", None),
            P(("row", "col"), None),
            P(),
            P("row", "col", None, None),
            P("row", "col", None, None),
            P("row", "col"),
        ),
        out_specs=P("col", None),
        check_vma=False,
    )
```

profile of v0, /device:TPU:8, one launch (start us, length us, event | category | flops | bytes accessed | tf_op | source)
XLA Modules:
  0.0 170.9 jit_solution(14388593459501252930)
XLA Ops:
  0.0 0.0 copy-start
  0.0 0.9 fusion.15
  0.9 0.7 copy-done
  1.6 6.8 %convolution_bitcast_fusion = f32[2,512,256]{1,2,0:T(8,128)} fusion(bf16[2,8,512,256]{3,2,1,0:T(8,128)(2,1)} %param.9, bf16[8,512,256,1]{2,1,0,3:T(8,128)(2,1)S(1)} %bitcast.31, bf16[2,8,512,256]{3,2,1,0:T(8,128)(2,1)} %param.10, f32[2,8,256]{2,1,0:T(8,128)S(1)} %fusion.15), kind=kOutput, calls=%fused_computation.9 | convolution fusion | flops 2149580800 | bytes 11550720 | tf_op jit(solution)/shard_map/ajtk,ajks->ats/dot_general | solution.py:47
  8.4 0.0 copy-start.1
  8.4 0.0 copy-start.2
  8.4 1.6 copy.21
  10.0 40.9 %all_to_all.20 = f32[32,32,256]{2,1,0:T(8,128)} all-to-all(f32[32,32,256]{2,1,0:T(8,128)S(1)} %bitcast.33), channel_id=1, replica_groups=mesh['row'=8,'col'=32] {'col'}, dimensions={0} | all-to-all | bytes 2097152 | tf_op jit(solution)/shard_map/all_to_all | solution.py:14
  51.0 1.3 reduce_sum.18
  52.3 0.0 copy-done.1
  52.3 0.0 copy-done.2
  52.3 0.9 broadcast_in_dim.4
  53.2 3.9 %all-to-all-start.1 = ((bf16[32,32,256]{2,1,0:T(8,128)(2,1)}), bf16[32,32,256]{2,1,0:T(8,128)(2,1)S(1)}, u32[]{:S(2)}, u32[]{:S(2)}) async-start(bf16[32,32,256]{2,1,0:T(8,128)(2,1)} %broadcast_in_dim.4), calls=%async_computation.1 | async-start | bytes 1048576 | tf_op jit(solution)/shard_map/all_to_all | solution.py:26
  57.1 19.1 %all-to-all-done.1 = bf16[32,32,256]{2,1,0:T(8,128)(2,1)S(1)} async-done(((bf16[32,32,256]{2,1,0:T(8,128)(2,1)}), bf16[32,32,256]{2,1,0:T(8,128)(2,1)S(1)}, u32[]{:S(2)}, u32[]{:S(2)}) %all-to-all-start.1) | async-done | bytes 524320 | tf_op jit(solution)/shard_map/all_to_all | solution.py:26
  76.2 7.8 %fusion.5 = f32[8,512,256]{1,2,0:T(8,128)} fusion(bf16[2,8,512,256]{3,2,1,0:T(8,128)(2,1)} %param.10, bf16[2,512,256,1]{2,1,0,3:T(8,128)(2,1)S(1)} %bitcast.34, bf16[2,8,512,256]{3,2,1,0:T(8,128)(2,1)} %param.9, f32[2,8,256]{2,0,1:T(2,128)S(1)} %copy.24), kind=kOutput, calls=%fused_computation.7 | convolution fusion | flops 2149580800 | bytes 13123584 | tf_op jit(solution)/shard_map/ajtk,ajks->jts/dot_general | solution.py:55
  83.9 53.6 %all_to_all.21 = f32[8,512,256]{1,2,0:T(8,128)} all-to-all(f32[8,512,256]{1,2,0:T(8,128)} %fusion.5), channel_id=1, replica_groups=mesh['row'=8,'col'=32] {'row'}, dimensions={0} | all-to-all | bytes 8388608 | tf_op jit(solution)/shard_map/all_to_all | solution.py:14
  137.5 2.7 %reduce_sum.19 = bf16[512,256]{0,1:T(8,128)(2,1)S(1)} reduce(f32[8,512,256]{1,2,0:T(8,128)} %all_to_all.21, f32[]{:T(128)} %constant.0.clone.1), dimensions={0}, to_apply=%region_1.0 | reduce | flops 917504 | bytes 4456452 | tf_op jit(solution)/shard_map/reduce_sum | solution.py:15
  140.2 0.1 copy.26
  140.4 0.1 broadcast_in_dim.5
  140.5 29.1 %all_to_all.22 = bf16[8,512,256]{2,1,0:T(8,128)(2,1)S(1)} all-to-all(bf16[8,512,256]{2,1,0:T(8,128)(2,1)S(1)} %broadcast_in_dim.5), channel_id=1, replica_groups=mesh['row'=8,'col'=32] {'row'}, dimensions={0} | all-to-all | bytes 4194304 | tf_op jit(solution)/shard_map/all_to_all | solution.py:26
  169.6 1.3 copy.46
  (2 shorter events, 0.0 us)
Async XLA Ops:
  0.0 1.6 copy-start
  8.4 43.8 %copy-start.1 = (bf16[32,256]{1,0:T(8,128)(2,1)S(1)}, bf16[32,256]{1,0:T(8,128)(2,1)}, u32[]{:S(2)}) copy-start(bf16[32,256]{1,0:T(8,128)(2,1)} %param.7) | copy-start | bytes 49156
  8.4 43.8 %copy-start.2 = (f32[256]{0:T(256)S(1)}, f32[256]{0:T(256)}, u32[]{:S(2)}) copy-start(f32[256]{0:T(256)} %param.8) | copy-start | bytes 3076
  53.2 23.0 %all-to-all-start.1 = ((bf16[32,32,256]{2,1,0:T(8,128)(2,1)}), bf16[32,32,256]{2,1,0:T(8,128)(2,1)S(1)}, u32[]{:S(2)}, u32[]{:S(2)}) async-start(bf16[32,32,256]{2,1,0:T(8,128)(2,1)} %broadcast_in_dim.4), calls=%async_computation.1 | async-start | bytes 1048576 | tf_op jit(solution)/shard_map/all_to_all | solution.py:26
where the time goes:
time: 172 us; the launch traced here: 171 us
  blocking collectives  124 us (72%)
  waiting for transfers between devices  19.1 us (11%)
  matrix products  14.6 us (8%)
  other arithmetic  4.9 us (3%)
  local copies, waits for them, and re-layouts  4.75 us (3%)
  starting transfers between devices  3.89 us (2%)
    all_to_all x2, blocking collectives, sent_and_summed(): lax.all_to_all(blocks, axis, split_axis=0, concat_axis=0, tiled=True)  94.5 us
    all_to_all x1, blocking collectives, sent_to_all(): return lax.all_to_all(copies, axis, split_axis=0, concat_axis=0, tiled=True)  29.1 us
    all_to_all x1, waiting for transfers between devices, sent_to_all(): return lax.all_to_all(copies, axis, split_axis=0, concat_axis=0, tiled=True)  19.1 us
    dot_general x1, matrix products, local(): jnp.einsum('ajtk,ajks->jts', v_coef, adjoint, preferred_element_type=jnp....  7.78 us
    dot_general x1, matrix products, local(): jnp.einsum('ajtk,ajks->ats', u_coef, coeffs, preferred_element_type=jnp.f...  6.82 us
    reduce_sum x2, other arithmetic, sent_and_summed(): return arrived.sum(axis=0)  3.99 us
    all_to_all x1, starting transfers between devices, sent_to_all(): return lax.all_to_all(copies, axis, split_axis=0, concat_axis=0, tiled=True)  3.89 us
  transfers between devices with their start and end apart: 1, of which 1 were waited for; matrix products, arithmetic and copies ran while one was open for 0% of the time, Pallas kernels for 0%

commit v1 on v0

v1 whole, which is shorter than its diff:
```python
import functools

import jax
import jax.numpy as jnp
from jax import lax
from jax.experimental import pallas as pl
from jax.experimental.pallas import tpu as pltpu
from jax.sharding import PartitionSpec as P

MESH = pl.DeviceIdType.MESH
F32, BF16 = jnp.float32, jnp.bfloat16

CHUNKS = (
    (0, 512, (0, 1, 2)),
    (512, 512, (1, 2, 0)),
    (1024, 512, (2, 0, 1)),
    (1536, 512, (0, 1, 2)),
    (2048, 512, (1, 2, 0)),
    (2560, 512, (2, 0, 1)),
    (3072, 384, (0, 1, 2)),
    (3712, 384, (1, 2, 0)),
    (3456, 256, (2, 0, 1)),
)
READY = {0: (0,), 1: (1,), 2: (2,), 3: (3,), 4: (4,), 5: (5,), 6: (6,), 7: (7, 8)}
OFFSETS = tuple((dx, dz) for dx in (2, 1, 3, 0) for dz in (2, 1, 3, 0) if (dx, dz) != (0, 0))


def matmul(a, b):
    return lax.dot_general(a, b, (((1,), (0,)), ((), ())), preferred_element_type=F32)


def matmul_t(a, b):
    return lax.dot_general(a, b, (((1,), (1,)), ((), ())), preferred_element_type=F32)


def event_order(n):
    events = []
    for i in range(n):
        wave = i // 3
        for stage in range(6):
            events.append((stage * 3 + wave * 3 + (2 if stage > 2 else 0), stage, i))
    return [(stage, i) for _, stage, i in sorted(events)]


def kernel(
    x_hbm, obs_hbm, sat_hbm, u_hbm, v_hbm, ranks_hbm, out,
    xb, ub, vb, obs, sat, ranks, xt, part, recv_core, send_a, recv_a, resid, resid_t, grad,
    send1, send2, send3, recv1, recv2, recv3,
    load_sem, small_sem, core_send, core_recv, a_send, a_recv, b_send, b_recv, row_send, row_recv,
):
    r, c = lax.axis_index("row"), lax.axis_index("col")
    y, zl = r // 2, r % 2
    x, zh, k = c // 8, (c % 8) // 2, c % 2
    here = x * 4 + zh
    tile_rows, tile_cols = ub.shape[0], ub.shape[1]

    row_peer = (
        (y * 2 + 1 - zl, c),
        ((y + 1 - 2 * (y % 2)) * 2 + zl, c),
        ((3 - y) * 2 + zl, c),
    )
    bits = (zl, ((y + 1) // 2) % 2, y // 2)
    core_peer = (r, c + 1 - 2 * k)

    def chip_at(dx, dz):
        return ((x + dx) % 4) * 4 + (zh + dz) % 4

    barrier = pltpu.get_barrier_semaphore()
    peers = [core_peer, *row_peer] + [(r, chip_at(dx, dz) * 2 + k) for dx, dz in OFFSETS]
    for peer in peers:
        pl.semaphore_signal(barrier, inc=1, device_id=peer, device_id_type=MESH)

    def v_load(a, j):
        return pltpu.make_async_copy(v_hbm.at[a, j], vb.at[a, j], load_sem.at[0, a * tile_cols + j])

    def u_load(a, j):
        return pltpu.make_async_copy(u_hbm.at[a, j], ub.at[a, j], load_sem.at[1, a * tile_cols + j])

    def x_load(j):
        return pltpu.make_async_copy(x_hbm.at[pl.ds(j * 512, 512)], xb.at[j], load_sem.at[2, j])

    small = (
        pltpu.make_async_copy(ranks_hbm, ranks, small_sem.at[0]),
        pltpu.make_async_copy(obs_hbm, obs, small_sem.at[1]),
        pltpu.make_async_copy(sat_hbm, sat, small_sem.at[2]),
    )
    small[0].start()
    for j in range(tile_cols):
        x_load(j).start()
        v_load(0, j).start()
        u_load(0, j).start()
    for j in range(tile_cols):
        v_load(1, j).start()
        u_load(1, j).start()
    small[1].start()
    small[2].start()

    eye = (
        lax.broadcasted_iota(jnp.int32, (256, 256), 0) == lax.broadcasted_iota(jnp.int32, (256, 256), 1)
    ).astype(F32).astype(BF16)
    lane = lax.broadcasted_iota(jnp.int32, (256, 256), 1)

    def masked(value, a, j):
        return jnp.where(lane < ranks[a, j], value, 0.0).astype(BF16)

    small[0].wait()
    core_copies = []
    for a in range(tile_rows):
        for j in range(tile_cols):
            if a == 0:
                x_load(j).wait()
                xt[j] = matmul_t(eye, xb[j]).astype(BF16)
            v_load(a, j).wait()
            coeffs = masked(matmul(xt[j], vb[a, j]), a, j)
            u_load(a, j).wait()
            term = matmul_t(ub[a, j], coeffs).reshape(8, 2, 32, 256)
            if j == 0:
                part[pl.ds(a * 8, 8)] = term
            else:
                part[pl.ds(a * 8, 8)] += term
        if a == 0:
            pl.semaphore_wait(barrier, len(peers))
        copy = pltpu.make_async_remote_copy(
            src_ref=part.at[pl.ds(a * 8, 8), 1 - k],
            dst_ref=recv_core.at[pl.ds(a * 8, 8)],
            send_sem=core_send.at[a],
            recv_sem=core_recv.at[a],
            device_id=core_peer,
            device_id_type=MESH,
        )
        copy.start()
        core_copies.append(copy)

    for a in range(tile_rows):
        core_copies[a].wait_recv()
        blocks = pl.ds(a * 8, 8)
        send_a[blocks] = (part[blocks, k] + recv_core[blocks]).astype(BF16)

    a_copies = []
    for n, (dx, dz) in enumerate(OFFSETS):
        there = chip_at(dx, dz)
        copy = pltpu.make_async_remote_copy(
            src_ref=send_a.at[there],
            dst_ref=recv_a.at[n],
            send_sem=a_send.at[n],
            recv_sem=a_recv.at[n],
            device_id=(r, there * 2 + k),
            device_id_type=MESH,
        )
        copy.start()
        a_copies.append(copy)

    small[1].wait()
    small[2].wait()
    predicted = part[here, k] + recv_core[here]
    for n, copy in enumerate(a_copies):
        copy.wait_recv()
        predicted = predicted + recv_a[n].astype(F32)
    scale = sat[...].reshape(1, 256)
    misfit = (predicted - obs[...].astype(F32)) / scale
    resid[here, k] = (scale * jnp.tanh(misfit)).astype(BF16)

    b_copies = []
    for n, (dx, dz) in enumerate(OFFSETS):
        copy = pltpu.make_async_remote_copy(
            src_ref=resid.at[here, k],
            dst_ref=resid.at[here, k],
            send_sem=b_send.at[n],
            recv_sem=b_recv.at[n],
            device_id=(r, chip_at(dx, dz) * 2 + k),
            device_id_type=MESH,
        )
        copy.start()
        b_copies.append(copy)
    for copy in core_copies + a_copies:
        copy.wait_send()
    for copy in b_copies:
        copy.wait_recv()
    copy = pltpu.make_async_remote_copy(
        src_ref=resid.at[:, k],
        dst_ref=resid.at[:, k],
        send_sem=core_send.at[2],
        recv_sem=core_recv.at[2],
        device_id=core_peer,
        device_id_type=MESH,
    )
    copy.start()
    for other in b_copies:
        other.wait_send()
    copy.wait()

    for a in range(tile_rows):
        resid_t[a] = matmul_t(eye, resid[pl.ds(a * 8, 8)].reshape(512, 256)).astype(BF16)

    sends = [(send1, recv1), (send2, recv2), (send3, recv3)]

    def base_of(i, depth):
        first, rows, dims = CHUNKS[i]
        base = first
        for d in range(depth):
            base = base + bits[dims[d]] * (rows >> (d + 1))
        return base if depth == 0 else pl.multiple_of(base, 16)

    def reduce_copy(i, step):
        first, rows, dims = CHUNKS[i]
        slot = pl.ds(first >> (step + 1), rows >> (step + 1))
        return pltpu.make_async_remote_copy(
            src_ref=sends[step][0].at[slot],
            dst_ref=sends[step][1].at[slot],
            send_sem=row_send.at[i, step],
            recv_sem=row_recv.at[i, step],
            device_id=row_peer[dims[step]],
            device_id_type=MESH,
        )

    def gather_copy(i, step):
        first, rows, dims = CHUNKS[i]
        where = pl.ds(base_of(i, step + 1), rows >> (step + 1))
        return pltpu.make_async_remote_copy(
            src_ref=out.at[where],
            dst_ref=out.at[where],
            send_sem=row_send.at[i, 3 + step],
            recv_sem=row_recv.at[i, 3 + step],
            device_id=row_peer[dims[step]],
            device_id_type=MESH,
        )

    def send_part(i, step):
        first, rows, dims = CHUNKS[i]
        half = rows >> (step + 1)
        bit = bits[dims[step]]
        theirs = pl.multiple_of((1 - bit) * half, 16)
        base = base_of(i, step)
        value = grad[pl.ds(pl.multiple_of(base + theirs, 16), half)]
        slot = first >> (step + 1)
        if step > 0:
            value = value + sends[step - 1][1][pl.ds(pl.multiple_of((first >> step) + theirs, 16), half)].astype(F32)
        sends[step][0][pl.ds(slot, half)] = value.astype(BF16)
        reduce_copy(i, step).start()
        if step > 0:
            mine = pl.multiple_of(bit * half, 16)
            keep = pl.ds(pl.multiple_of(base + mine, 16), half)
            grad[keep] = grad[keep] + sends[step - 1][1][
                pl.ds(pl.multiple_of((first >> step) + mine, 16), half)
            ].astype(F32)

    for j in range(tile_cols):
        total = None
        for a in range(tile_rows):
            adjoint = masked(matmul(resid_t[a], ub[a, j]), a, j)
            term = matmul_t(vb[a, j], adjoint)
            total = term if total is None else total + term
        grad[pl.ds(j * 512, 512)] = total
        for i in READY[j]:
            send_part(i, 0)

    for stage, i in event_order(len(CHUNKS)):
        first, rows, dims = CHUNKS[i]
        if stage < 2:
            reduce_copy(i, stage).wait_recv()
            send_part(i, stage + 1)
        elif stage == 2:
            reduce_copy(i, 2).wait_recv()
            where = pl.ds(base_of(i, 3), rows >> 3)
            out[where] = (grad[where] + recv3[pl.ds(first >> 3, rows >> 3)].astype(F32)).astype(BF16)
            gather_copy(i, 2).start()
        else:
            step = 5 - stage
            gather_copy(i, step).wait_recv()
            if step > 0:
                gather_copy(i, step - 1).start()
    for i in range(len(CHUNKS)):
        for step in range(3):
            reduce_copy(i, step).wait_send()
            gather_copy(i, step).wait_send()


def local(x_field, observed, sat_scale, u_coef, v_coef, ranks):
    tile_rows, tile_cols, width, cap = u_coef.shape
    sources = x_field.shape[1]
    hbm = pl.BlockSpec(memory_space=pltpu.HBM)
    chunks = len(CHUNKS)
    peers = len(OFFSETS)
    dma = pltpu.SemaphoreType.DMA
    half_rows = tile_cols * width // 2
    return pl.pallas_call(
        kernel,
        out_shape=jax.ShapeDtypeStruct(x_field.shape, BF16),
        in_specs=[hbm] * 6,
        out_specs=pl.BlockSpec(memory_space=pltpu.VMEM),
        scratch_shapes=[
            pltpu.VMEM((tile_cols, width, sources), BF16),
            pltpu.VMEM(u_coef.shape, BF16),
            pltpu.VMEM(v_coef.shape, BF16),
            pltpu.VMEM(observed.shape, BF16),
            pltpu.VMEM(sat_scale.shape, F32),
            pltpu.SMEM(ranks.shape, jnp.int32),
            pltpu.VMEM((tile_cols, sources, width), BF16),
            pltpu.VMEM((16, 2, 32, sources), F32),
            pltpu.VMEM((16, 32, sources), F32),
            pltpu.VMEM((16, 32, sources), BF16),
            pltpu.VMEM((peers, 32, sources), BF16),
            pltpu.VMEM((16, 2, 32, sources), BF16),
            pltpu.VMEM((tile_rows, sources, width), BF16),
            pltpu.VMEM((tile_cols * width, sources), F32),
            pltpu.VMEM((half_rows, sources), BF16),
            pltpu.VMEM((half_rows // 2, sources), BF16),
            pltpu.VMEM((half_rows // 4, sources), BF16),
            pltpu.VMEM((half_rows, sources), BF16),
            pltpu.VMEM((half_rows // 2, sources), BF16),
            pltpu.VMEM((half_rows // 4, sources), BF16),
            dma((3, tile_rows * tile_cols)),
            dma((3,)),
            dma((3,)),
            dma((3,)),
            dma((peers,)),
            dma((peers,)),
            dma((peers,)),
            dma((peers,)),
            dma((chunks, 6)),
            dma((chunks, 6)),
        ],
        compiler_params=pltpu.CompilerParams(
            collective_id=0, has_side_effects=True, vmem_limit_bytes=60 * 2**20
        ),
        name="redatum",
    )(x_field, observed, sat_scale, u_coef, v_coef, ranks)


def solution(mesh):
    return jax.shard_map(
        local,
        mesh=mesh,
        in_specs=(
            P("col", None),
            P(("row", "col"), None),
            P(),
            P("row", "col", None, None),
            P("row", "col", None, None),
            P("row", "col"),
        ),
        out_specs=P("col", None),
        check_vma=False,
    )
```

time: 172 us -> 77.9 us (0.45)
  blocking collectives: 124 us -> 0 us
  Pallas kernels: 0 us -> 74.7 us
  waiting for transfers between devices: 19.1 us -> 0 us
  matrix products: 14.6 us -> 0 us
  other arithmetic: 4.9 us -> 0 us
  starting transfers between devices: 3.89 us -> 0 us
    all_to_all x3 -> x0, blocking collectives: 124 us -> none  [the longest x2 94.5 us: sent_and_summed(): lax.all_to_all(blocks, axis, split_axis=0, concat_axis=0, tiled=True)]
    pallas_call x0 -> x1, Pallas kernels: none -> 74.7 us  [local(): pl.pallas_call(kernel, out_shape=jax.ShapeDtypeStruct(x_field.shape, BF16...]
    all_to_all x1 -> x0, waiting for transfers between devices: 19.1 us -> none  [sent_to_all(): return lax.all_to_all(copies, axis, split_axis=0, concat_axis=0, tiled=True)]
    dot_general x2 -> x0, matrix products: 14.6 us -> none  [the longest x1 7.78 us: local(): jnp.einsum('ajtk,ajks->jts', v_coef, adjoint, preferred_element_type=jnp....]
    reduce_sum x2 -> x0, other arithmetic: 3.99 us -> none  [sent_and_summed(): return arrived.sum(axis=0)]
    all_to_all x1 -> x0, starting transfers between devices: 3.89 us -> none  [sent_to_all(): return lax.all_to_all(copies, axis, split_axis=0, concat_axis=0, tiled=True)]
  transfers between devices with their start and end apart: 1 -> 0, of which waited for: 1 -> 0; matrix products, arithmetic and copies ran while one was open for 0% -> 0% of each run, Pallas kernels for 0% -> 0%
where the time goes in v1:
time: 77.9 us; the launch traced here: 77.8 us
  Pallas kernels  74.7 us (96%)
  local copies, waits for them, and re-layouts  3.05 us (4%)
    pallas_call x1, Pallas kernels, local(): pl.pallas_call(kernel, out_shape=jax.ShapeDtypeStruct(x_field.shape, BF16...  74.7 us
    unnamed x1, local copies, waits for them, and re-layouts  3.05 us

profile of v1, /device:TPU:8, one launch (start us, length us, event | category | flops | bytes accessed | tf_op | source)
XLA Modules:
  0.0 77.8 jit_solution(300955391811418670)
XLA Ops:
  0.0 74.7 %redatum.1 = bf16[4096,256]{1,0:T(8,128)(2,1)} custom-call(bf16[4096,256]{1,0:T(8,128)(2,1)} %x_hbm.1, bf16[32,256]{1,0:T(8,128)(2,1)} %obs_hbm.1, f32[256]{0:T(256)} %sat_hbm.1, bf16[2,8,512,256]{3,2,1,0:T(8,128)(2,1)} %u_hbm.1, bf16[2,8,512,256]{3,2,1,0:T(8,128)(2,1)} %v_hbm.1, s32[2,8]{1,0:T(2,128)} %ranks_hbm.1), custom_call_target="tpu_custom_call" | custom-call | tf_op jit(solution)/shard_map/redatum/pallas_call | solution.py:286
  74.8 3.0 %copy.8 = bf16[4096,256]{1,0:T(8,128)(2,1)} copy(bf16[4096,256]{1,0:T(8,128)(2,1)} %redatum.1) | data formatting | bytes 4194304

commit v2 on v1

--- a/solution.py
+++ b/solution.py
@@ -10,18 +10,44 @@
 MESH = pl.DeviceIdType.MESH
 F32, BF16 = jnp.float32, jnp.bfloat16
 
-CHUNKS = (
-    (0, 512, (0, 1, 2)),
-    (512, 512, (1, 2, 0)),
-    (1024, 512, (2, 0, 1)),
-    (1536, 512, (0, 1, 2)),
-    (2048, 512, (1, 2, 0)),
-    (2560, 512, (2, 0, 1)),
-    (3072, 384, (0, 1, 2)),
-    (3712, 384, (1, 2, 0)),
-    (3456, 256, (2, 0, 1)),
-)
-READY = {0: (0,), 1: (1,), 2: (2,), 3: (3,), 4: (4,), 5: (5,), 6: (6,), 7: (7, 8)}
+ORDERS = ((0, 1, 2), (1, 2, 0), (2, 0, 1))
+UNIT = 128
+
+
+def chunk_table(rows):
+    sizes = [2 * UNIT] * (rows // (2 * UNIT) - 1) + [UNIT, UNIT]
+    table, first = [], 0
+    for i, size in enumerate(sizes):
+        table.append((first, size, ORDERS[i % 3]))
+        first += size
+    return table
+
+
+def event_order(chunks, rate=46.65e3, latency=2.6, row_bytes=512):
+    free, arrivals = [0.0] * 3, {}
+
+    def send(i, stage, now):
+        _, rows, dims = chunks[i]
+        step = stage if stage < 3 else 5 - stage
+        d = dims[step]
+        free[d] = max(free[d], now) + (rows >> (step + 1)) * row_bytes / rate
+        arrivals[stage, i] = free[d] + latency
+
+    now, order = 0.0, []
+    for i, (first, rows, _) in enumerate(chunks):
+        now = max(now, 0.4 + 0.26 * ((first + rows - 1) // 512))
+        send(i, 0, now)
+    while arrivals:
+        stage, i = min(arrivals, key=lambda e: (arrivals[e], e))
+        now = max(now, arrivals.pop((stage, i))) + 0.05
+        if stage < 3:
+            now += (chunks[i][1] >> (stage + 1)) * 0.0009
+        order.append((stage, i))
+        if stage < 5:
+            send(i, stage + 1, now)
+    return order
+
+
 OFFSETS = tuple((dx, dz) for dx in (2, 1, 3, 0) for dz in (2, 1, 3, 0) if (dx, dz) != (0, 0))
 
 
@@ -33,20 +59,12 @@
     return lax.dot_general(a, b, (((1,), (1,)), ((), ())), preferred_element_type=F32)
 
 
-def event_order(n):
-    events = []
-    for i in range(n):
-        wave = i // 3
-        for stage in range(6):
-            events.append((stage * 3 + wave * 3 + (2 if stage > 2 else 0), stage, i))
-    return [(stage, i) for _, stage, i in sorted(events)]
-
-
 def kernel(
     x_hbm, obs_hbm, sat_hbm, u_hbm, v_hbm, ranks_hbm, out,
-    xb, ub, vb, obs, sat, ranks, xt, part, recv_core, send_a, recv_a, resid, resid_t, grad,
+    xb, ub, vb, obs, sat, ranks, xt, ct, part, recv_core, send_a, recv_a, resid, resid_t, grad,
     send1, send2, send3, recv1, recv2, recv3,
-    load_sem, small_sem, core_send, core_recv, a_send, a_recv, b_send, b_recv, row_send, row_recv,
+    load_sem, small_sem, core_send, core_recv, a_send, a_recv, b_send, b_recv, r_send, r_recv,
+    row_send, row_recv,
 ):
     r, c = lax.axis_index("row"), lax.axis_index("col")
     y, zl = r // 2, r % 2
@@ -70,28 +88,27 @@
     for peer in peers:
         pl.semaphore_signal(barrier, inc=1, device_id=peer, device_id_type=MESH)
 
-    def v_load(a, j):
-        return pltpu.make_async_copy(v_hbm.at[a, j], vb.at[a, j], load_sem.at[0, a * tile_cols + j])
-
-    def u_load(a, j):
-        return pltpu.make_async_copy(u_hbm.at[a, j], ub.at[a, j], load_sem.at[1, a * tile_cols + j])
-
-    def x_load(j):
-        return pltpu.make_async_copy(x_hbm.at[pl.ds(j * 512, 512)], xb.at[j], load_sem.at[2, j])
-
+    def load(n, a, p):
+        tiles = pl.ds(p * 2, 2)
+        if n == 2:
+            return pltpu.make_async_copy(
+                x_hbm.at[pl.ds(p * 1024, 1024)], xb.at[pl.ds(p * 1024, 1024)], load_sem.at[2, 0, p]
+            )
+        source, target = ((v_hbm, vb), (u_hbm, ub))[n]
+        return pltpu.make_async_copy(source.at[a, tiles], target.at[a, tiles], load_sem.at[n, a, p])
+
+    pieces = tile_cols // 2
+    xs = [load(2, 0, p) for p in range(pieces)]
+    vs = [load(0, a, p) for a in range(tile_rows) for p in range(pieces)]
+    us = [load(1, a, p) for a in range(tile_rows) for p in range(pieces)]
     small = (
         pltpu.make_async_copy(ranks_hbm, ranks, small_sem.at[0]),
         pltpu.make_async_copy(obs_hbm, obs, small_sem.at[1]),
         pltpu.make_async_copy(sat_hbm, sat, small_sem.at[2]),
     )
     small[0].start()
-    for j in range(tile_cols):
-        x_load(j).start()
-        v_load(0, j).start()
-        u_load(0, j).start()
-    for j in range(tile_cols):
-        v_load(1, j).start()
-        u_load(1, j).start()
+    for copy in xs + vs + us:
+        copy.start()
     small[1].start()
     small[2].start()
 
@@ -103,21 +120,24 @@
     def masked(value, a, j):
         return jnp.where(lane < ranks[a, j], value, 0.0).astype(BF16)
 
-    small[0].wait()
+    for copy in (small[0], *xs, *vs):
+        copy.wait()
+    for j in range(tile_cols):
+        xt[j] = matmul_t(eye, xb[pl.ds(j * 512, 512)]).astype(BF16)
+    for j in range(tile_cols):
+        for a in range(tile_rows):
+            ct[a, j] = masked(matmul(xt[j], vb[a, j]), a, j)
+    for copy in us:
+        copy.wait()
     core_copies = []
     for a in range(tile_rows):
-        for j in range(tile_cols):
-            if a == 0:
-                x_load(j).wait()
-                xt[j] = matmul_t(eye, xb[j]).astype(BF16)
-            v_load(a, j).wait()
-            coeffs = masked(matmul(xt[j], vb[a, j]), a, j)
-            u_load(a, j).wait()
-            term = matmul_t(ub[a, j], coeffs).reshape(8, 2, 32, 256)
+        blocks = pl.ds(a * 8, 8)
+        for j in range(0, tile_cols, 2):
+            term = (matmul_t(ub[a, j], ct[a, j]) + matmul_t(ub[a, j + 1], ct[a, j + 1])).reshape(8, 2, 32, 256)
             if j == 0:
-                part[pl.ds(a * 8, 8)] = term
+                part[blocks] = term
             else:
-                part[pl.ds(a * 8, 8)] += term
+                part[blocks] += term
         if a == 0:
             pl.semaphore_wait(barrier, len(peers))
         copy = pltpu.make_async_remote_copy(
@@ -131,12 +151,11 @@
         copy.start()
         core_copies.append(copy)
 
+    a_copies = []
     for a in range(tile_rows):
         core_copies[a].wait_recv()
         blocks = pl.ds(a * 8, 8)
         send_a[blocks] = (part[blocks, k] + recv_core[blocks]).astype(BF16)
-
-    a_copies = []
     for n, (dx, dz) in enumerate(OFFSETS):
         there = chip_at(dx, dz)
         copy = pltpu.make_async_remote_copy(
@@ -174,35 +193,42 @@
         b_copies.append(copy)
     for copy in core_copies + a_copies:
         copy.wait_send()
-    for copy in b_copies:
-        copy.wait_recv()
-    copy = pltpu.make_async_remote_copy(
-        src_ref=resid.at[:, k],
-        dst_ref=resid.at[:, k],
-        send_sem=core_send.at[2],
-        recv_sem=core_recv.at[2],
-        device_id=core_peer,
-        device_id_type=MESH,
-    )
-    copy.start()
+    r_copies = []
+    for dx in (0, 1, 3, 2):
+        for n, offset in enumerate(OFFSETS):
+            if offset[0] == (4 - dx) % 4:
+                b_copies[n].wait_recv()
+        blocks = pl.ds(((x + dx) % 4) * 4, 4)
+        copy = pltpu.make_async_remote_copy(
+            src_ref=resid.at[blocks, k],
+            dst_ref=resid.at[blocks, k],
+            send_sem=r_send.at[dx],
+            recv_sem=r_recv.at[dx],
+            device_id=core_peer,
+            device_id_type=MESH,
+        )
+        copy.start()
+        r_copies.append(copy)
     for other in b_copies:
         other.wait_send()
-    copy.wait()
+    for copy in r_copies:
+        copy.wait()
 
     for a in range(tile_rows):
         resid_t[a] = matmul_t(eye, resid[pl.ds(a * 8, 8)].reshape(512, 256)).astype(BF16)
 
+    chunks = chunk_table(grad.shape[0])
     sends = [(send1, recv1), (send2, recv2), (send3, recv3)]
 
     def base_of(i, depth):
-        first, rows, dims = CHUNKS[i]
+        first, rows, dims = chunks[i]
         base = first
         for d in range(depth):
             base = base + bits[dims[d]] * (rows >> (d + 1))
         return base if depth == 0 else pl.multiple_of(base, 16)
 
     def reduce_copy(i, step):
-        first, rows, dims = CHUNKS[i]
+        first, rows, dims = chunks[i]
         slot = pl.ds(first >> (step + 1), rows >> (step + 1))
         return pltpu.make_async_remote_copy(
             src_ref=sends[step][0].at[slot],
@@ -214,7 +240,7 @@
         )
 
     def gather_copy(i, step):
-        first, rows, dims = CHUNKS[i]
+        first, rows, dims = chunks[i]
         where = pl.ds(base_of(i, step + 1), rows >> (step + 1))
         return pltpu.make_async_remote_copy(
             src_ref=out.at[where],
@@ -226,7 +252,7 @@
         )
 
     def send_part(i, step):
-        first, rows, dims = CHUNKS[i]
+        first, rows, dims = chunks[i]
         half = rows >> (step + 1)
         bit = bits[dims[step]]
         theirs = pl.multiple_of((1 - bit) * half, 16)
@@ -244,6 +270,7 @@
                 pl.ds(pl.multiple_of((first >> step) + mine, 16), half)
             ].astype(F32)
 
+    sent = 0
     for j in range(tile_cols):
         total = None
         for a in range(tile_rows):
@@ -251,11 +278,12 @@
             term = matmul_t(vb[a, j], adjoint)
             total = term if total is None else total + term
         grad[pl.ds(j * 512, 512)] = total
-        for i in READY[j]:
-            send_part(i, 0)
-
-    for stage, i in event_order(len(CHUNKS)):
-        first, rows, dims = CHUNKS[i]
+        while sent < len(chunks) and chunks[sent][0] + chunks[sent][1] <= (j + 1) * 512:
+            send_part(sent, 0)
+            sent += 1
+
+    for stage, i in event_order(chunks):
+        first, rows, dims = chunks[i]
         if stage < 2:
             reduce_copy(i, stage).wait_recv()
             send_part(i, stage + 1)
@@ -269,17 +297,18 @@
             gather_copy(i, step).wait_recv()
             if step > 0:
                 gather_copy(i, step - 1).start()
-    for i in range(len(CHUNKS)):
+    for i in range(len(chunks)):
         for step in range(3):
             reduce_copy(i, step).wait_send()
             gather_copy(i, step).wait_send()
 
 
 def local(x_field, observed, sat_scale, u_coef, v_coef, ranks):
+    arrays = (x_field, observed, sat_scale, u_coef, v_coef, ranks)
     tile_rows, tile_cols, width, cap = u_coef.shape
     sources = x_field.shape[1]
     hbm = pl.BlockSpec(memory_space=pltpu.HBM)
-    chunks = len(CHUNKS)
+    chunks = len(chunk_table(x_field.shape[0]))
     peers = len(OFFSETS)
     dma = pltpu.SemaphoreType.DMA
     half_rows = tile_cols * width // 2
@@ -289,13 +318,14 @@
         in_specs=[hbm] * 6,
         out_specs=pl.BlockSpec(memory_space=pltpu.VMEM),
         scratch_shapes=[
-            pltpu.VMEM((tile_cols, width, sources), BF16),
+            pltpu.VMEM(x_field.shape, BF16),
             pltpu.VMEM(u_coef.shape, BF16),
             pltpu.VMEM(v_coef.shape, BF16),
             pltpu.VMEM(observed.shape, BF16),
             pltpu.VMEM(sat_scale.shape, F32),
             pltpu.SMEM(ranks.shape, jnp.int32),
             pltpu.VMEM((tile_cols, sources, width), BF16),
+            pltpu.VMEM((tile_rows, tile_cols, sources, cap), BF16),
             pltpu.VMEM((16, 2, 32, sources), F32),
             pltpu.VMEM((16, 32, sources), F32),
             pltpu.VMEM((16, 32, sources), BF16),
@@ -309,22 +339,24 @@
             pltpu.VMEM((half_rows, sources), BF16),
             pltpu.VMEM((half_rows // 2, sources), BF16),
             pltpu.VMEM((half_rows // 4, sources), BF16),
-            dma((3, tile_rows * tile_cols)),
+            dma((3, tile_rows, tile_cols // 2)),
             dma((3,)),
-            dma((3,)),
-            dma((3,)),
+            dma((tile_rows,)),
+            dma((tile_rows,)),
             dma((peers,)),
             dma((peers,)),
             dma((peers,)),
             dma((peers,)),
+            dma((4,)),
+            dma((4,)),
             dma((chunks, 6)),
             dma((chunks, 6)),
         ],
         compiler_params=pltpu.CompilerParams(
-            collective_id=0, has_side_effects=True, vmem_limit_bytes=60 * 2**20
+            collective_id=0, has_side_effects=True, vmem_limit_bytes=36 * 2**20
         ),
         name="redatum",
-    )(x_field, observed, sat_scale, u_coef, v_coef, ranks)
+    )(*(pltpu.with_memory_space_constraint(array, pltpu.HBM) for array in arrays))
 
 
 def solution(mesh):

time: 77.9 us -> 69.3 us (0.89)
  Pallas kernels: 74.7 us -> 67.8 us
  local copies, waits for them, and re-layouts: 3.05 us -> 1.32 us
    pallas_call x1, Pallas kernels: 74.7 us -> 67.8 us  [local(): pl.pallas_call(kernel, out_shape=jax.ShapeDtypeStruct(x_field.shape, BF16...]
    unnamed x1, local copies, waits for them, and re-layouts: 3.05 us -> 1.32 us
where the time goes in v2:
time: 69.3 us; the launch traced here: 69.1 us
  Pallas kernels  67.8 us (98%)
  local copies, waits for them, and re-layouts  1.32 us (2%)
    pallas_call x1, Pallas kernels, local(): pl.pallas_call(kernel, out_shape=jax.ShapeDtypeStruct(x_field.shape, BF16...  67.8 us

profile of v2, /device:TPU:8, one launch (start us, length us, event | category | flops | bytes accessed | tf_op | source)
XLA Modules:
  0.0 69.1 jit_solution(11966345446828995121)
XLA Ops:
  0.0 67.8 %redatum.1 = bf16[4096,256]{1,0:T(8,128)(2,1)S(1)} custom-call(bf16[4096,256]{1,0:T(8,128)(2,1)} %x_hbm.1, bf16[32,256]{1,0:T(8,128)(2,1)} %obs_hbm.1, f32[256]{0:T(256)} %sat_hbm.1, bf16[2,8,512,256]{3,2,1,0:T(8,128)(2,1)} %u_hbm.1, bf16[2,8,512,256]{3,2,1,0:T(8,128)(2,1)} %v_hbm.1, s32[2,8]{1,0:T(2,128)} %ranks_hbm.1), custom_call_target="tpu_custom_call" | custom-call | tf_op jit(solution)/shard_map/redatum/pallas_call | solution.py:315
  67.8 1.3 %copy.8 = bf16[4096,256]{1,0:T(8,128)(2,1)} copy(bf16[4096,256]{1,0:T(8,128)(2,1)S(1)} %redatum.1) | data formatting | bytes 4194304
